TPU v7x, 32 devices: a whole 2x2x4 slice. The times are simulated.
32 devices in a mesh: dp: 16 (over z, y, core), tensor: 2 (over x).
Axes of the slice: x: 2, y: 2, z: 4, core: 2. Of those that a mesh axis runs over, the one named last changes fastest.
Arguments:
- activations: bfloat16 [4096, 27648], P('dp', 'tensor'), may hold values from -6 to 6
- output_gradient: bfloat16 [4096, 5120], P('dp', 'tensor'), may hold values from -6 to 6
- adapter_a: bfloat16 [2, 13824, 128], P('tensor', 'dp'), may hold values from -0.0390625 to 0.0390625
- adapter_b: bfloat16 [128, 5120], P(None, 'tensor'), may hold values from -0.078125 to 0.078125
- log_ratio: float32 [4096], P('dp'), may hold values from -1.5 to 1.5
- lengths: int32 [1, 16], replicated, may hold values from 1 to 256, as said below
- rewards: int32 [1, 16], replicated, may hold values from 0 to 10
Outputs:
- grad_a: float32 [2, 13824, 128], P('tensor', 'dp')
- adapter_b_gradient: float32 [128, 5120], P(None, 'tensor')
- loss: float32 [], replicated
Inputs may be any that keep to these rules, and one draw needn't show every extreme that they name: `lengths`: in every group some rollout has length 256.
All inputs are finite; a program needn't handle non-finite values.
Results may differ from a plain program's by a relative error of at most 0.0067.
Values may be sent and summed in bfloat16 or wider, within the bound.
A program may use at most 64 MiB of HBM per device.

v0:
```python
import jax
import jax.numpy as jnp
from jax import lax
from jax.sharding import PartitionSpec as P

clip_eps = 0.2
adapter_scale_factor = 2.0


def token_terms(length_row, reward_row, log_ratio, offset):
    reward = reward_row.astype(jnp.float32)
    center = jnp.mean(reward)
    spread = jnp.mean((reward - center) * (reward - center))
    advantage = (reward - center) / jnp.sqrt(spread + 1.0)
    ends = jnp.cumsum(length_row)
    starts = ends - length_row
    slots = jnp.arange(log_ratio.shape[0], dtype=jnp.int32) + offset
    member = ((slots[None, :] >= starts[:, None]) & (slots[None, :] < ends[:, None])).astype(
        jnp.float32
    )
    live = jnp.sum(member, axis=0)
    token_adv = jnp.sum(member * advantage[:, None], axis=0)
    ratio = jnp.exp(log_ratio)
    unclipped = ratio * token_adv
    clipped = jnp.clip(ratio, 1.0 - clip_eps, 1.0 + clip_eps) * token_adv
    token_loss = -jnp.minimum(unclipped, clipped)
    slope = jnp.where(unclipped <= clipped, -unclipped, jnp.zeros_like(unclipped))
    return (live * slope, jnp.sum(live * token_loss), jnp.sum(live))


def local(activations, output_gradient, adapter_a, adapter_b, log_ratio, lengths, rewards):
    tokens = activations.shape[0]
    groups = lengths.shape[0]
    per_group = lax.axis_size("dp") // groups
    position = lax.axis_index("dp")
    group_id = position // per_group
    offset = position % per_group * tokens
    length_row = lax.dynamic_index_in_dim(lengths, group_id, 0, keepdims=False)
    reward_row = lax.dynamic_index_in_dim(rewards, group_id, 0, keepdims=False)
    token_coefficient, loss_local, live_count = token_terms(
        length_row, reward_row, log_ratio, offset
    )
    columns = activations
    partial_low = jnp.dot(
        columns,
        lax.all_gather(adapter_a, "dp", axis=1, tiled=True)[0],
        preferred_element_type=jnp.float32,
    )
    partial_back = lax.dot_general(
        output_gradient, adapter_b, (((1,), (1,)), ((), ())), preferred_element_type=jnp.float32
    )
    low_rank, backward_projection = lax.psum((partial_low, partial_back), "tensor")
    error_rows = (adapter_scale_factor * token_coefficient[:, None] * backward_projection).astype(
        jnp.bfloat16
    )
    weighted_error = token_coefficient[:, None] * low_rank
    local_adapter_b_gradient = adapter_scale_factor * jnp.einsum(
        "tr,td->rd",
        weighted_error,
        output_gradient.astype(jnp.float32),
        precision=lax.Precision.HIGHEST,
    )
    columns = activations
    grad_a = lax.psum_scatter(
        lax.dot_general(
            columns, error_rows, (((0,), (0,)), ((), ())), preferred_element_type=jnp.float32
        ),
        "dp",
        scatter_dimension=0,
        tiled=True,
    )
    grad_b_sum, loss_sum, live_sum = lax.psum(
        (local_adapter_b_gradient, loss_local, live_count), "dp"
    )
    factor = groups / live_sum
    return ((factor * grad_a)[None], factor * grad_b_sum, factor * loss_sum)


def solution(mesh):
    in_specs = (
        P("dp", "tensor"),
        P("dp", "tensor"),
        P("tensor", "dp", None),
        P(None, "tensor"),
        P("dp"),
        P(),
        P(),
    )
    out_specs = (P("tensor", "dp", None), P(None, "tensor"), P())
    return jax.shard_map(local, mesh=mesh, in_specs=in_specs, out_specs=out_specs, check_vma=False)
```

profile of v0, /device:TPU:0, one launch (start us, length us, event | category | flops | bytes accessed | tf_op | source)
XLA Modules:
  0.0 290.5 jit_solution(11864515134774246795)
XLA Ops:
  7.2 0.0 copy-start
  7.2 0.0 all-gather.2.cloned.1.call-start
  7.2 0.7 all-gather.2.cloned.1.call-update
  7.9 0.0 all-reduce.7.cloned.1.call-start
  8.0 1.3 convert_reduce_fusion.2
  9.9 1.3 multiply_reduce_fusion.1
  11.8 0.7 copy.16
  12.6 0.1 reduce.3
  12.7 0.7 divide_bitcast_fusion
  13.4 0.7 bitcast_subtract_fusion
  14.1 0.0 copy-done
  14.1 2.2 fusion.7
  16.3 0.0 copy-start.2
  16.3 43.8 %all-gather.2.cloned.1.call-done = bf16[1,13824,128]{2,1,0:T(8,128)(2,1)} async-done(((bf16[1,864,128]{2,1,0:T(8,128)(2,1)}), bf16[1,13824,128]{2,1,0:T(8,128)(2,1)}) %all-gather.2.cloned.1.call-update) | async-done | bytes 3538960 | tf_op jit(solution)/shard_map/all_gather | solution.py:46
  60.2 6.7 %fusion = f32[256,128]{1,0:T(8,128)} fusion(bf16[256,13824]{1,0:T(8,128)(2,1)} %param.7, bf16[1,13824,128]{2,1,0:T(8,128)(2,1)} %all-gather.2.cloned.1.call-done), kind=kOutput, calls=%fused_computation.2 | convolution fusion | flops 905969664 | bytes 10747904 | tf_op jit(solution)/shard_map/dot_general | solution.py:44
  66.8 0.0 all-reduce.7.cloned.1.call-update
  66.9 0.0 all-reduce.5.cloned.1.call-start
  66.9 0.7 convert_reduce_fusion.1
  67.6 0.0 copy-done.2
  67.6 0.6 broadcast_multiply_fusion.1
  68.2 20.8 %all-reduce.7.cloned.1.call-done = (f32[256,128]{1,0:T(8,128)}, f32[256,128]{1,0:T(8,128)}) async-done(((f32[256,128]{1,0:T(8,128)}, f32[256,128]{1,0:T(8,128)}), (f32[256,128]{1,0:T(8,128)}, f32[256,128]{1,0:T(8,128)})) %all-reduce.7.cloned.1.call-update) | async-done | bytes 262160 | tf_op jit(solution)/shard_map/psum | solution.py:52
  88.9 2.7 convolution_multiply_fusion
  91.7 0.0 copy-start.1
  91.7 0.0 all-reduce.5.cloned.1.call-update
  91.7 0.0 reduce-scatter.4.cloned.1.call-start
  91.8 0.8 copy-done.1
  92.6 7.2 %convolution_bitcast_fusion = f32[13824,128]{0,1:T(8,128)} fusion(bf16[256,13824]{1,0:T(8,128)(2,1)} %param.7, f32[256,128]{1,0:T(8,128)S(1)} %copy-done.1, f32[256]{0:T(256)S(1)} %get-tuple-element.22), kind=kOutput, calls=%fused_computation | convolution fusion | flops 906035200 | bytes 14287872 | tf_op jit(solution)/shard_map/dot_general | solution.py:65
  99.8 8.4 %copy.18 = f32[13824,128]{1,0:T(8,128)} copy(f32[13824,128]{0,1:T(8,128)} %convolution_bitcast_fusion) | data formatting | bytes 14155776
  108.2 0.0 reduce-scatter.4.cloned.1.call-update
  108.2 33.6 %all-reduce = (f32[]{:T(128)}, f32[]{:T(128)}) all-reduce(f32[]{:T(128)} %get-tuple-element.15, f32[]{:T(128)} %get-tuple-element.24), channel_id=1, replica_groups=mesh['dp'=16,'tensor'=2] {'dp'}, use_global_device_ids=true, to_apply=%region_2.3 | all-reduce | flops 2 | bytes 16 | tf_op jit(solution)/shard_map/psum | solution.py:72
  143.1 44.0 %all-reduce.5.cloned.1.call-done = f32[128,2560]{1,0:T(8,128)} async-done(((f32[128,2560]{1,0:T(8,128)}), f32[128,2560]{1,0:T(8,128)}) %all-reduce.5.cloned.1.call-update) | async-done | bytes 1310736 | tf_op jit(solution)/shard_map/psum | solution.py:72
  187.1 2.5 broadcast_multiply_fusion
  189.6 91.1 %reduce-scatter.4.cloned.1.call-done = f32[864,128]{1,0:T(8,128)} async-done(((f32[13824,128]{1,0:T(8,128)}), f32[864,128]{1,0:T(8,128)}) %reduce-scatter.4.cloned.1.call-update) | async-done | bytes 442384
  280.6 1.2 copy.19
  281.9 1.0 copy.17
  (3 shorter events, 0.1 us)
Async XLA Ops:
  7.2 6.9 %copy-start = (bf16[256,2560]{1,0:T(8,128)(2,1)S(1)}, bf16[256,2560]{1,0:T(8,128)(2,1)}, u32[]{:S(2)}) copy-start(bf16[256,2560]{1,0:T(8,128)(2,1)} %param.8) | copy-start | bytes 3932164
  7.2 53.0 %all-gather.2.cloned.1.call-start = ((), (), s32[]{:S(2)}) async-start(), calls=%async_computation.1 | async-start | bytes 3760128 | tf_op jit(solution)/shard_map/all_gather | solution.py:46
  7.9 81.0 %all-reduce.7.cloned.1.call-start = ((), (), s32[]{:S(2)}) async-start(), calls=%async_computation.4 | async-start | bytes 524288 | tf_op jit(solution)/shard_map/psum | solution.py:52
  16.3 51.3 %copy-start.2 = (f32[256]{0:T(256)S(1)}, f32[256]{0:T(256)}, u32[]{:S(2)}) copy-start(f32[256]{0:T(256)} %param.11) | copy-start | bytes 3076
  66.9 120.3 %all-reduce.5.cloned.1.call-start = ((), (), s32[]{:S(2)}) async-start(), calls=%async_computation.2 | async-start | bytes 2621440 | tf_op jit(solution)/shard_map/psum | solution.py:72
  91.7 0.9 copy-start.1
  91.7 188.9 %reduce-scatter.4.cloned.1.call-start = ((), (), s32[]{:S(2)}) async-start(), calls=%async_computation.3 | async-start | bytes 7520256
Sparse Core Ops, SparseCore 0:
  10.3 49.8 all-gather.1
  67.0 21.9 all-reduce.6
  93.0 94.0 all-reduce.4
  191.0 89.6 reduce-scatter.3
where the time goes:
time: 291 us
  waiting for transfers between devices  200 us (69%)
  blocking collectives  33.6 us (12%)
  matrix products  18.8 us (6%)
  between operations  17.6 us (6%)
  local copies, waits for them, and re-layouts  12.2 us (4%)
  other arithmetic  7.82 us (3%)
    unnamed x5, waiting for transfers between devices  91.8 us
    psum x1, waiting for transfers between devices, local(): lax.psum((local_adapter_b_gradient, loss_local, live_count), 'dp')  44 us
    all_gather x1, waiting for transfers between devices, local(): lax.all_gather(adapter_a, 'dp', axis=1, tiled=True)[0]  43.8 us
    psum x1, blocking collectives, local(): lax.psum((local_adapter_b_gradient, loss_local, live_count), 'dp')  33.6 us
    psum x1, waiting for transfers between devices, local(): lax.psum((partial_low, partial_back), 'tensor')  20.8 us
    unnamed x9, local copies, waits for them, and re-layouts  11.4 us
    dot_general x1, matrix products, local(): lax.dot_general(columns, error_rows, (((0,), (0,)), ((), ())), preferred_...  7.15 us
    dot_general x1, matrix products, local(): jnp.dot(columns, lax.all_gather(adapter_a, 'dp', axis=1, tiled=True)[0],...  6.66 us
  transfers between devices with their start and end apart: 4, of which 4 were waited for; matrix products, arithmetic and copies ran while one was open for 9% of the time, Pallas kernels for 0%

commit v1 on v0

--- a/solution.py
+++ b/solution.py
@@ -43,7 +43,9 @@
     columns = activations
     partial_low = jnp.dot(
         columns,
-        lax.all_gather(adapter_a, "dp", axis=1, tiled=True)[0],
+        jnp.concatenate(
+            lax.all_to_all(jnp.stack([adapter_a] * lax.axis_size("dp")), "dp", 0, 0), axis=1
+        )[0],
         preferred_element_type=jnp.float32,
     )
     partial_back = lax.dot_general(

time: 291 us -> 329 us (1.13)
  waiting for transfers between devices: 200 us -> 232 us
  starting transfers between devices: 0.16 us -> 7.72 us
    all_to_all x0 -> x1, waiting for transfers between devices: none -> 62.1 us  [local(): lax.all_to_all(jnp.stack([adapter_a] * lax.axis_size('dp')), 'dp', 0, 0)]
    all_gather x1 -> x0, waiting for transfers between devices: 43.8 us -> none  [local(): lax.all_gather(adapter_a, 'dp', axis=1, tiled=True)[0]]
    psum x1, waiting for transfers between devices: 20.8 us -> 34.6 us  [local(): lax.psum((partial_low, partial_back), 'tensor')]
    all_to_all x0 -> x1, starting transfers between devices: none -> 7.59 us  [local(): lax.all_to_all(jnp.stack([adapter_a] * lax.axis_size('dp')), 'dp', 0, 0)]
    unnamed x5 -> x4, waiting for transfers between devices: 91.8 us -> 91.2 us
    unnamed x9 -> x15, local copies, waits for them, and re-layouts: 11.4 us -> 11.5 us
  transfers between devices with their start and end apart: 4 -> 4, of which waited for: 4 -> 4; matrix products, arithmetic and copies ran while one was open for 9% -> 7% of each run, Pallas kernels for 0% -> 0%
where the time goes in v1:
time: 329 us; the launch traced here: 328 us
  waiting for transfers between devices  232 us (71%)
  blocking collectives  33.6 us (10%)
  matrix products  17.7 us (5%)
  between operations  17.7 us (5%)
  local copies, waits for them, and re-layouts  14.8 us (4%)
  starting transfers between devices  7.72 us (2%)
  other arithmetic  5.18 us (2%)
    unnamed x4, waiting for transfers between devices  91.2 us
    all_to_all x1, waiting for transfers between devices, local(): lax.all_to_all(jnp.stack([adapter_a] * lax.axis_size('dp')), 'dp', 0, 0)  62.1 us
    psum x1, waiting for transfers between devices, local(): lax.psum((local_adapter_b_gradient, loss_local, live_count), 'dp')  43.9 us
    psum x1, waiting for transfers between devices, local(): lax.psum((partial_low, partial_back), 'tensor')  34.6 us
    psum x1, blocking collectives, local(): lax.psum((local_adapter_b_gradient, loss_local, live_count), 'dp')  33.6 us
    unnamed x15, local copies, waits for them, and re-layouts  11.5 us
    all_to_all x1, starting transfers between devices, local(): lax.all_to_all(jnp.stack([adapter_a] * lax.axis_size('dp')), 'dp', 0, 0)  7.59 us
    dot_general x1, matrix products, local(): lax.dot_general(columns, error_rows, (((0,), (0,)), ((), ())), preferred_...  7.15 us
  transfers between devices with their start and end apart: 4, of which 4 were waited for; matrix products, arithmetic and copies ran while one was open for 7% of the time, Pallas kernels for 0%

profile of v1, /device:TPU:0, one launch (start us, length us, event | category | flops | bytes accessed | tf_op | source)
XLA Modules:
  0.0 328.5 jit_solution(12532151226707070565)
XLA Ops:
  7.2 0.0 copy-start
  7.2 3.3 %stack.2 = bf16[16,1,864,128]{3,2,1,0:T(8,128)(2,1)} broadcast(bf16[864,128]{1,0:T(8,128)(2,1)} %bitcast.18), dimensions={2,3} | broadcast | bytes 3760128 | tf_op jit(solution)/shard_map/stack | solution.py:47
  10.5 0.0 copy-start.5
  10.5 0.0 copy-start.4
  10.5 0.0 copy-start.1
  10.5 7.6 %all-to-all-start = ((bf16[16,1,864,128]{3,2,1,0:T(8,128)(2,1)}), bf16[16,1,864,128]{3,2,1,0:T(8,128)(2,1)}, u32[]{:S(2)}, u32[]{:S(2)}) async-start(bf16[16,1,864,128]{3,2,1,0:T(8,128)(2,1)} %stack.2), calls=%async_computation | async-start | bytes 7077888 | tf_op jit(solution)/shard_map/all_to_all | solution.py:47
  18.1 0.0 all-reduce.7.cloned.1.call-start
  18.1 0.0 copy-done.5
  18.2 0.6 convert_reduce_fusion.2
  19.4 0.6 multiply_reduce_fusion.1
  20.7 0.0 copy-done.4
  20.7 0.1 copy.16
  20.8 0.1 reduce.3
  21.0 0.0 copy-done
  21.0 0.0 copy-done.1
  21.0 1.2 fusion.5
  22.2 62.1 %all-to-all-done = bf16[16,1,864,128]{3,2,1,0:T(8,128)(2,1)} async-done(((bf16[16,1,864,128]{3,2,1,0:T(8,128)(2,1)}), bf16[16,1,864,128]{3,2,1,0:T(8,128)(2,1)}, u32[]{:S(2)}, u32[]{:S(2)}) %all-to-all-start) | async-done | bytes 3538976 | tf_op jit(solution)/shard_map/all_to_all | solution.py:47
  84.2 0.0 copy-start.3
  84.2 6.7 %fusion.6 = f32[256,128]{1,0:T(8,128)} fusion(bf16[256,13824]{1,0:T(8,128)(2,1)} %param.7, bf16[13824,128]{1,0:T(8,128)(2,1)} %bitcast.6), kind=kOutput, calls=%fused_computation.25 | convolution fusion | flops 905969664 | bytes 10747904 | tf_op jit(solution)/shard_map/dot_general | solution.py:44
  90.9 0.0 all-reduce.7.cloned.1.call-update
  90.9 0.0 all-reduce.5.cloned.1.call-start
  91.0 0.7 convert_reduce_fusion.1
  91.7 0.0 copy-done.3
  91.7 0.6 broadcast_multiply_fusion.1
  92.3 34.6 %all-reduce.7.cloned.1.call-done = (f32[256,128]{1,0:T(8,128)}, f32[256,128]{1,0:T(8,128)}) async-done(((f32[256,128]{1,0:T(8,128)}, f32[256,128]{1,0:T(8,128)}), (f32[256,128]{1,0:T(8,128)}, f32[256,128]{1,0:T(8,128)})) %all-reduce.7.cloned.1.call-update) | async-done | bytes 262160 | tf_op jit(solution)/shard_map/psum | solution.py:54
  126.8 2.7 convolution_multiply_fusion
  129.6 0.0 copy-start.2
  129.6 0.0 all-reduce.5.cloned.1.call-update
  129.6 0.0 reduce-scatter.4.cloned.1.call-start
  129.7 0.8 copy-done.2
  130.5 7.1 %convolution_bitcast_fusion = f32[13824,128]{0,1:T(8,128)} fusion(bf16[256,13824]{1,0:T(8,128)(2,1)} %param.7, f32[256,128]{1,0:T(8,128)S(1)} %copy-done.2, f32[256]{0:T(256)S(1)} %get-tuple-element.22), kind=kOutput, calls=%fused_computation | convolution fusion | flops 906035200 | bytes 14287872 | tf_op jit(solution)/shard_map/dot_general | solution.py:67
  137.6 8.4 %copy.18 = f32[13824,128]{1,0:T(8,128)} copy(f32[13824,128]{0,1:T(8,128)} %convolution_bitcast_fusion) | data formatting | bytes 14155776
  146.1 0.0 reduce-scatter.4.cloned.1.call-update
  146.1 33.6 %all-reduce = (f32[]{:T(128)}, f32[]{:T(128)}) all-reduce(f32[]{:T(128)} %get-tuple-element.15, f32[]{:T(128)} %get-tuple-element.24), channel_id=1, replica_groups=mesh['dp'=16,'tensor'=2] {'dp'}, use_global_device_ids=true, to_apply=%region_2.3 | all-reduce | flops 2 | bytes 16 | tf_op jit(solution)/shard_map/psum | solution.py:74
  181.0 43.9 %all-reduce.5.cloned.1.call-done = f32[128,2560]{1,0:T(8,128)} async-done(((f32[128,2560]{1,0:T(8,128)}), f32[128,2560]{1,0:T(8,128)}) %all-reduce.5.cloned.1.call-update) | async-done | bytes 1310736 | tf_op jit(solution)/shard_map/psum | solution.py:74
  224.9 2.5 broadcast_multiply_fusion
  227.4 91.2 %reduce-scatter.4.cloned.1.call-done = f32[864,128]{1,0:T(8,128)} async-done(((f32[13824,128]{1,0:T(8,128)}), f32[864,128]{1,0:T(8,128)}) %reduce-scatter.4.cloned.1.call-update) | async-done | bytes 442384
  318.6 1.2 copy.19
  319.9 1.0 copy.17
  (5 shorter events, 0.1 us)
Async XLA Ops:
  7.2 13.8 %copy-start = (bf16[256,2560]{1,0:T(8,128)(2,1)S(1)}, bf16[256,2560]{1,0:T(8,128)(2,1)}, u32[]{:S(2)}) copy-start(bf16[256,2560]{1,0:T(8,128)(2,1)} %param.8) | copy-start | bytes 3932164
  10.5 7.7 %copy-start.5 = (s32[1,16]{1,0:T(1,128)S(1)}, s32[1,16]{1,0:T(1,128)}, u32[]{:S(2)}) copy-start(s32[1,16]{1,0:T(1,128)} %param.13) | copy-start | bytes 196
  10.5 10.2 %copy-start.4 = (s32[1,16]{1,0:T(1,128)S(1)}, s32[1,16]{1,0:T(1,128)}, u32[]{:S(2)}) copy-start(s32[1,16]{1,0:T(1,128)} %param.12) | copy-start | bytes 196
  10.5 10.5 %copy-start.1 = (bf16[128,2560]{1,0:T(8,128)(2,1)S(1)}, bf16[128,2560]{1,0:T(8,128)(2,1)}, u32[]{:S(2)}) copy-start(bf16[128,2560]{1,0:T(8,128)(2,1)} %param.10) | copy-start | bytes 1966084
  10.5 73.7 %all-to-all-start = ((bf16[16,1,864,128]{3,2,1,0:T(8,128)(2,1)}), bf16[16,1,864,128]{3,2,1,0:T(8,128)(2,1)}, u32[]{:S(2)}, u32[]{:S(2)}) async-start(bf16[16,1,864,128]{3,2,1,0:T(8,128)(2,1)} %stack.2), calls=%async_computation | async-start | bytes 7077888 | tf_op jit(solution)/shard_map/all_to_all | solution.py:47
  18.1 108.7 %all-reduce.7.cloned.1.call-start = ((), (), s32[]{:S(2)}) async-start(), calls=%async_computation.4 | async-start | bytes 524288 | tf_op jit(solution)/shard_map/psum | solution.py:54
  84.2 7.4 %copy-start.3 = (f32[256]{0:T(256)S(1)}, f32[256]{0:T(256)}, u32[]{:S(2)}) copy-start(f32[256]{0:T(256)} %param.11) | copy-start | bytes 3076
  90.9 134.0 %all-reduce.5.cloned.1.call-start = ((), (), s32[]{:S(2)}) async-start(), calls=%async_computation.2 | async-start | bytes 2621440 | tf_op jit(solution)/shard_map/psum | solution.py:74
  129.6 0.9 copy-start.2
  129.6 189.0 %reduce-scatter.4.cloned.1.call-start = ((), (), s32[]{:S(2)}) async-start(), calls=%async_computation.3 | async-start | bytes 7520256
Sparse Core Ops, SparseCore 0:
  91.0 35.7 all-reduce.6
  130.9 94.0 all-reduce.4
  229.0 89.6 reduce-scatter.3
